TPU v7x, 32 devices: a whole 2x2x4 slice. The times are simulated.
32 devices in a mesh: lat: 4 (over y, x), lon: 8 (over z, core).
Axes of the slice: x: 2, y: 2, z: 4, core: 2. Of those that a mesh axis runs over, the one named last changes fastest.
Arguments:
- transport: bfloat16 [48, 512, 3072], P(None, 'lat', 'lon'), may hold values from -0.0625 to 0.0625
- sigma_class: int32 [48, 512, 3072], P(None, 'lat', 'lon'), may hold values from 0 to 199
- basin_id: int32 [512, 3072], P('lat', 'lon'), may hold values from 0 to 3
- depth_levels: int32 [512, 3072], P('lat', 'lon'), may hold values from 0 to 48
Outputs:
- overturning: bfloat16 [4, 200, 512], replicated
Inputs may be any that keep to these rules, and one draw needn't show every extreme that they name: `depth_levels`: 0 marks a land column.
All inputs are finite; a program needn't handle non-finite values.
Results may differ from a plain program's by a relative error of at most 0.001.
Values may be sent and summed in bfloat16 or wider, within the bound.
A program may use at most 64 MiB of HBM per device.

v0:
```python
import functools

import jax
import jax.numpy as jnp
import numpy as np
from jax import lax
from jax.experimental import pallas as pl
from jax.experimental.pallas import tpu as pltpu
from jax.sharding import PartitionSpec as P

CLASSES = 200
BASINS = 4
SUB = 8
LANES = 128
TILE = 256
STEP_ROWS = 16
MESH = pl.DeviceIdType.MESH
HIGHS = 26
HIGH_BLOCKS = 4


def hot_pairs(index, count, value):
    return [jnp.where(index == jnp.bfloat16(2 * i), value, jnp.bfloat16(0)) for i in range(count)]


def doubled(index):
    pair = jnp.concatenate([index, index - 1], axis=0)
    return pair.astype(jnp.float32).astype(jnp.bfloat16)


def squeeze_rows(product):
    rows = lax.broadcasted_iota(jnp.int32, (SUB, TILE), 0)
    lanes = lax.broadcasted_iota(jnp.int32, (SUB, TILE), 1)
    own = (lanes % SUB) == rows
    blocks = []
    for q in range(HIGH_BLOCKS):
        total = None
        for s in range(SUB):
            high = q * SUB + s
            if high * SUB >= CLASSES:
                break
            piece = jnp.where(own, product[high * SUB:(high + 1) * SUB, :], 0.0)
            piece = piece if s == 0 else pltpu.roll(piece, s, 1)
            total = piece if total is None else total + piece
        straight = jnp.where(rows == 0, total, 0.0)
        for r in range(1, SUB):
            straight = jnp.where(rows == r, pltpu.roll(total, TILE - r, 1), straight)
        blocks.append(straight)
    return jnp.concatenate(blocks, axis=1)


def bin_block(flow_ref, class_ref, basin_ref, depth_ref, out_ref, *accs):
    levels, _, cols = class_ref.shape
    chunks = cols // LANES
    per_trip = 24
    for half in range(STEP_ROWS // SUB):
        rows = slice(half * SUB, (half + 1) * SUB)

        def trip(t, carry, rows=rows):
            tiles = []
            for u in range(per_trip):
                level = t * per_trip + u
                for c in range(chunks):
                    lanes = slice(c * LANES, (c + 1) * LANES)
                    klass = class_ref[level, rows, lanes]
                    flow = flow_ref[level, :, lanes].astype(jnp.float32)[rows]
                    flow = jnp.where(level < depth_ref[rows, lanes], flow, 0.0)
                    high = doubled(klass >> 3)
                    low = doubled(basin_ref[rows, lanes] * SUB + (klass & 7))
                    value = jnp.concatenate([flow, flow], axis=0).astype(jnp.bfloat16)
                    tiles.append((
                        jnp.concatenate(hot_pairs(high, HIGHS // 2, value), axis=0),
                        jnp.concatenate(hot_pairs(low, TILE // (2 * SUB), jnp.bfloat16(1)), axis=0),
                    ))
            for k in range(0, len(tiles), 2):
                mxu, stage = (k // 2) % 2, (k // 4) % 2
                left = jnp.concatenate([tiles[k][0], tiles[k + 1][0]], axis=1)
                right = jnp.concatenate([tiles[k][1], tiles[k + 1][1]], axis=1)
                pltpu.matmul_push_rhs(right, staging_register=stage, mxu_index=mxu, transpose=True)
                pltpu.matmul_acc_lhs(accs[mxu], left, load_staged_rhs=stage)
            return carry

        lax.fori_loop(0, levels // per_trip, trip, 0)
        product = pltpu.matmul_pop(accs[0]) + pltpu.matmul_pop(accs[1])
        out_ref[rows, :] = squeeze_rows(product)


def bin_kernel(*refs):
    shape = (HIGHS * SUB, TILE)
    pl.run_scoped(
        functools.partial(bin_block, *refs), *[pltpu.ACC(m)(shape, jnp.float32) for m in (0, 1)]
    )


def bin_rows(transport, sigma_class, basin_id, depth_levels):
    levels, row_count, cols = sigma_class.shape
    deep = pl.BlockSpec((levels, STEP_ROWS, cols), lambda i: (0, i, 0))
    flat = pl.BlockSpec((STEP_ROWS, cols), lambda i: (i, 0))
    width = HIGH_BLOCKS * TILE
    return pl.pallas_call(
        bin_kernel,
        grid=(row_count // STEP_ROWS,),
        in_specs=[deep, deep, flat, flat],
        out_specs=pl.BlockSpec((STEP_ROWS, width), lambda i: (i, 0)),
        out_shape=jax.ShapeDtypeStruct((row_count, width), jnp.float32),
        name="bin_rows",
    )(transport, sigma_class, basin_id, depth_levels)


def running_sums():
    row = np.arange(HIGH_BLOCKS * LANES)
    column = np.arange(2 * TILE)
    lane = row % LANES
    klass = (row // LANES) * 64 + (lane % SUB) * SUB + (lane % 64) // SUB
    same = (lane // 64)[:, None] == (column // TILE)[None, :]
    return (same & (klass[:, None] <= (column % TILE)[None, :])).astype(jnp.bfloat16)


def accumulate(share, sums):
    pieces = []
    for pair in range(BASINS // 2):
        lanes = [share[:, q * TILE + pair * LANES:q * TILE + (pair + 1) * LANES] for q in range(HIGH_BLOCKS)]
        rest = jnp.concatenate(lanes, axis=1)
        total = None
        for _ in range(3):
            part = rest.astype(jnp.bfloat16)
            rest = rest - part.astype(jnp.float32)
            term = jnp.dot(part, sums, preferred_element_type=jnp.float32)
            total = term if total is None else total + term
        pieces.append(total)
    return jnp.concatenate(pieces, axis=1)


def share_kernel(lats, lons, table_ref, sums_ref, out_ref, half, acc, arrived, sums, sum_sem,
                 half_send, half_recv, arr_send, arr_recv, out_send, out_recv):
    lat, lon = lax.axis_index("lat"), lax.axis_index("lon")
    zs = lons // 2
    z, core = lon // 2, lax.rem(lon, 2)
    partner = (lat, z * 2 + (1 - core))
    z_peers = [(lat, lax.rem(z + k, zs) * 2 + core) for k in range(1, zs)]
    lat_peers = [(lax.rem(lat + k, lats), lon) for k in range(1, lats)]

    load = pltpu.make_async_copy(sums_ref, sums, sum_sem)
    load.start()
    barrier = pltpu.get_barrier_semaphore()
    everyone = [partner] + z_peers + lat_peers
    for peer in everyone:
        pl.semaphore_signal(barrier, inc=1, device_id=peer, device_id_type=MESH)
    pl.semaphore_wait(barrier, len(everyone))

    def send(src, dst, send_sem, recv_sem, peer):
        copy = pltpu.make_async_remote_copy(
            src_ref=src, dst_ref=dst, send_sem=send_sem, recv_sem=recv_sem,
            device_id=peer, device_id_type=MESH,
        )
        copy.start()
        return copy

    swaps = []
    for k in [*range(1, zs), 0]:
        d = lax.rem(z + k, zs)
        swaps.append((k, send(table_ref.at[2 * d + (1 - core)], half.at[k], half_send.at[k], half_recv.at[k], partner)))
    moves = []
    for k, swap in swaps:
        swap.wait_recv()
        d = lax.rem(z + k, zs)
        acc[k] = table_ref[2 * d + core] + half[k]
        if k > 0:
            moves.append(send(acc.at[k], arrived.at[k - 1], arr_send.at[k - 1], arr_recv.at[k - 1], z_peers[k - 1]))
    share = acc[0]
    for k in range(1, zs):
        moves[k - 1].wait_recv()
        share = share + arrived[k - 1]
    load.wait()
    me = lat * lons + lon
    out_ref[me] = accumulate(share, sums[...]).astype(jnp.bfloat16)

    copies = []

    def spread(owner, peer):
        n = len(copies)
        copies.append(send(out_ref.at[owner], out_ref.at[owner], out_send.at[n], out_recv.at[owner], peer))

    def landed(owner):
        pltpu.make_async_remote_copy(
            src_ref=out_ref.at[owner], dst_ref=out_ref.at[owner], send_sem=out_send.at[0],
            recv_sem=out_recv.at[owner], device_id=partner, device_id_type=MESH,
        ).wait_recv()

    for peer in z_peers + lat_peers:
        spread(me, peer)
    spread(me, partner)
    for k in range(1, zs):
        owner = lat * lons + lax.rem(z - k + zs, zs) * 2 + core
        landed(owner)
        for peer in lat_peers + [partner]:
            spread(owner, peer)
    for j in range(zs):
        for k in range(1, lats):
            owner = lax.rem(lat - k + lats, lats) * lons + lax.rem(z - j + zs, zs) * 2 + core
            landed(owner)
            spread(owner, partner)
    for j in range(zs):
        for k in range(lats):
            landed(lax.rem(lat - k + lats, lats) * lons + lax.rem(z - j + zs, zs) * 2 + (1 - core))
    for _, swap in swaps:
        swap.wait_send()
    for move in moves:
        move.wait_send()
    for copy in copies:
        copy.wait_send()


def share_rows(lats, lons, table):
    rows = table.shape[0] // lons
    width = table.shape[1]
    zs = lons // 2
    sends = (zs - 1) + (lats - 1) + 1 + (zs - 1) * lats + zs * (lats - 1)
    dma = pltpu.SemaphoreType.DMA
    return pl.pallas_call(
        functools.partial(share_kernel, lats, lons),
        out_shape=jax.ShapeDtypeStruct((lats * lons, rows, width), jnp.bfloat16),
        in_specs=[pl.BlockSpec(memory_space=pltpu.VMEM), pl.BlockSpec(memory_space=pl.ANY)],
        out_specs=pl.BlockSpec(memory_space=pltpu.VMEM),
        scratch_shapes=[
            pltpu.VMEM((zs, rows, width), jnp.float32),
            pltpu.VMEM((zs, rows, width), jnp.float32),
            pltpu.VMEM((zs - 1, rows, width), jnp.float32),
            pltpu.VMEM((HIGH_BLOCKS * LANES, 2 * TILE), jnp.bfloat16),
            dma(()),
            dma((zs,)), dma((zs,)), dma((zs - 1,)), dma((zs - 1,)),
            dma((sends,)), dma((lats * lons,)),
        ],
        compiler_params=pltpu.CompilerParams(collective_id=0, has_side_effects=True),
        name="share_rows",
    )(table.reshape(lons, rows, width), jnp.asarray(running_sums()))


def body(lats, lons, transport, sigma_class, basin_id, depth_levels):
    table = bin_rows(transport, sigma_class, basin_id, depth_levels)
    whole = share_rows(lats, lons, table).reshape(-1, BASINS, TILE)
    return jnp.transpose(whole[:, :, :CLASSES], (1, 2, 0))


def solution(mesh):
    placed = (P(None, "lat", "lon"), P(None, "lat", "lon"), P("lat", "lon"), P("lat", "lon"))
    local = functools.partial(body, mesh.shape["lat"], mesh.shape["lon"])
    return jax.shard_map(local, mesh=mesh, in_specs=placed, out_specs=P(), check_vma=False)
```

profile of v0, /device:TPU:0, one launch (start us, length us, event | category | flops | bytes accessed | tf_op | source)
XLA Modules:
  0.0 86.1 jit_solution(6979963579146115431)
XLA Ops:
  0.0 55.1 %bin_rows.1 = f32[128,1024]{1,0:T(8,128)} custom-call(bf16[48,128,384]{2,1,0:T(8,128)(2,1)} %refs_0_.1, s32[48,128,384]{2,1,0:T(8,128)} %refs_1_.1, s32[128,384]{1,0:T(8,128)} %refs_2_.1, s32[128,384]{1,0:T(8,128)} %refs_3_.1), custom_call_target="tpu_custom_call" | custom-call | tf_op jit(solution)/shard_map/bin_rows/pallas_call | solution.py:100
  55.1 27.7 %share_rows.1 = bf16[32,16,1024]{2,1,0:T(8,128)(2,1)} custom-call(f32[8,16,1024]{2,1,0:T(8,128)} %bitcast.4, bf16[512,512]{1,0:T(8,128)(2,1)} %constant.2.clone.sums_ref), custom_call_target="tpu_custom_call" | custom-call | tf_op jit(solution)/shard_map/share_rows/pallas_call | solution.py:220
  82.8 1.9 %reshape.7 = bf16[512,4,256]{2,1,0:T(4,128)(2,1)S(1)} reshape(bf16[32,16,1024]{2,1,0:T(8,128)(2,1)} %share_rows.1) | data formatting | bytes 2097152 | tf_op jit(solution)/shard_map/reshape | solution.py:241
  84.7 1.4 %copy.7 = bf16[512,4,200]{0,2,1:T(8,128)(2,1)} copy(bf16[512,4,200]{2,1,0:T(4,128)(2,1)S(1)} %bitcast.3) | data formatting | bytes 1638400
where the time goes:
time: 86.3 us; the launch traced here: 86.1 us
  Pallas kernels  82.8 us (96%)
  local copies, waits for them, and re-layouts  3.27 us (4%)
    pallas_call x1, Pallas kernels, bin_rows(): pl.pallas_call(bin_kernel, grid=(row_count // STEP_ROWS,), in_specs=[deep...  55.1 us
    pallas_call x1, Pallas kernels, share_rows(): pl.pallas_call(functools.partial(share_kernel, lats, lons), out_shape=jax...  27.7 us
    reshape x1, local copies, waits for them, and re-layouts, body(): whole = share_rows(lats, lons, table).reshape(-1, BASINS, TILE)  1.86 us

commit v1 on v0

--- a/solution.py
+++ b/solution.py
@@ -17,15 +17,19 @@
 MESH = pl.DeviceIdType.MESH
 HIGHS = 26
 HIGH_BLOCKS = 4
-
-
-def hot_pairs(index, count, value):
-    return [jnp.where(index == jnp.bfloat16(2 * i), value, jnp.bfloat16(0)) for i in range(count)]
-
-
-def doubled(index):
-    pair = jnp.concatenate([index, index - 1], axis=0)
-    return pair.astype(jnp.float32).astype(jnp.bfloat16)
+ONE_HOT = jnp.float8_e4m3fn
+
+
+def high_rows(high, value):
+    pair = jnp.concatenate([high, high - 1], axis=0).astype(jnp.int16)
+    zero = jnp.bfloat16(0)
+    return jnp.concatenate([jnp.where(pair == jnp.int16(i), value, zero) for i in range(0, HIGHS, 2)], axis=0)
+
+
+def low_rows(low):
+    four = jnp.concatenate([low - i for i in range(4)], axis=0).astype(jnp.int8)
+    one, zero = ONE_HOT(1), ONE_HOT(0)
+    return jnp.concatenate([jnp.where(four == jnp.int8(i), one, zero) for i in range(0, TILE // SUB, 4)], axis=0)
 
 
 def squeeze_rows(product):
@@ -65,13 +69,9 @@
                     klass = class_ref[level, rows, lanes]
                     flow = flow_ref[level, :, lanes].astype(jnp.float32)[rows]
                     flow = jnp.where(level < depth_ref[rows, lanes], flow, 0.0)
-                    high = doubled(klass >> 3)
-                    low = doubled(basin_ref[rows, lanes] * SUB + (klass & 7))
                     value = jnp.concatenate([flow, flow], axis=0).astype(jnp.bfloat16)
-                    tiles.append((
-                        jnp.concatenate(hot_pairs(high, HIGHS // 2, value), axis=0),
-                        jnp.concatenate(hot_pairs(low, TILE // (2 * SUB), jnp.bfloat16(1)), axis=0),
-                    ))
+                    low = basin_ref[rows, lanes] * SUB + (klass & 7)
+                    tiles.append((high_rows(klass >> 3, value), low_rows(low)))
             for k in range(0, len(tiles), 2):
                 mxu, stage = (k // 2) % 2, (k // 4) % 2
                 left = jnp.concatenate([tiles[k][0], tiles[k + 1][0]], axis=1)
@@ -113,25 +113,35 @@
     lane = row % LANES
     klass = (row // LANES) * 64 + (lane % SUB) * SUB + (lane % 64) // SUB
     same = (lane // 64)[:, None] == (column // TILE)[None, :]
-    return (same & (klass[:, None] <= (column % TILE)[None, :])).astype(jnp.bfloat16)
-
-
-def accumulate(share, sums):
-    pieces = []
+    return (same & (klass[:, None] <= (column % TILE)[None, :])).astype(ONE_HOT)
+
+
+def accumulate(share, sums, acc0, acc1):
+    parts = []
     for pair in range(BASINS // 2):
         lanes = [share[:, q * TILE + pair * LANES:q * TILE + (pair + 1) * LANES] for q in range(HIGH_BLOCKS)]
         rest = jnp.concatenate(lanes, axis=1)
-        total = None
         for _ in range(3):
-            part = rest.astype(jnp.bfloat16)
-            rest = rest - part.astype(jnp.float32)
-            term = jnp.dot(part, sums, preferred_element_type=jnp.float32)
-            total = term if total is None else total + term
-        pieces.append(total)
+            part = rest.astype(jnp.bfloat16).astype(jnp.float32)
+            rest = rest - part
+            parts.append(part)
+    left = jnp.concatenate(parts, axis=0).astype(jnp.bfloat16)
+    rows = share.shape[0]
+    for k in range(2):
+        for n, acc in enumerate((acc0, acc1)):
+            right = sums[k * TILE:(k + 1) * TILE, n * TILE:(n + 1) * TILE]
+            pltpu.matmul_push_rhs(right, staging_register=k, mxu_index=n)
+            pltpu.matmul_acc_lhs(acc, left[:, k * TILE:(k + 1) * TILE], load_staged_rhs=k)
+    pieces = []
+    halves = [pltpu.matmul_pop(acc0), pltpu.matmul_pop(acc1)]
+    for pair in range(BASINS // 2):
+        for total in halves:
+            three = [total[(pair * 3 + i) * rows:(pair * 3 + i + 1) * rows] for i in range(3)]
+            pieces.append(three[0] + three[1] + three[2])
     return jnp.concatenate(pieces, axis=1)
 
 
-def share_kernel(lats, lons, table_ref, sums_ref, out_ref, half, acc, arrived, sums, sum_sem,
+def share_kernel(lats, lons, table_ref, sums_ref, final_ref, out_ref, half, acc, arrived, sums, sum_sem,
                  half_send, half_recv, arr_send, arr_recv, out_send, out_recv):
     lat, lon = lax.axis_index("lat"), lax.axis_index("lon")
     zs = lons // 2
@@ -173,7 +183,12 @@
         share = share + arrived[k - 1]
     load.wait()
     me = lat * lons + lon
-    out_ref[me] = accumulate(share, sums[...]).astype(jnp.bfloat16)
+
+    def cumulative(acc0, acc1):
+        out_ref[me] = accumulate(share, sums[...], acc0, acc1).astype(jnp.bfloat16)
+
+    shape = (6 * share.shape[0], TILE)
+    pl.run_scoped(cumulative, *[pltpu.ACC(m)(shape, jnp.float32) for m in (0, 1)])
 
     copies = []
 
@@ -203,6 +218,12 @@
     for j in range(zs):
         for k in range(lats):
             landed(lax.rem(lat - k + lats, lats) * lons + lax.rem(z - j + zs, zs) * 2 + (1 - core))
+    rows = lons * share.shape[0]
+    for group in range(lats):
+        for basin in range(BASINS):
+            block = out_ref[group * lons:(group + 1) * lons, :, basin * TILE:(basin + 1) * TILE]
+            turned = jnp.transpose(block.reshape(rows, TILE))
+            final_ref[basin, :, group * rows:(group + 1) * rows] = turned[:CLASSES]
     for _, swap in swaps:
         swap.wait_send()
     for move in moves:
@@ -219,14 +240,15 @@
     dma = pltpu.SemaphoreType.DMA
     return pl.pallas_call(
         functools.partial(share_kernel, lats, lons),
-        out_shape=jax.ShapeDtypeStruct((lats * lons, rows, width), jnp.bfloat16),
+        out_shape=jax.ShapeDtypeStruct((BASINS, CLASSES, lats * lons * rows), jnp.bfloat16),
         in_specs=[pl.BlockSpec(memory_space=pltpu.VMEM), pl.BlockSpec(memory_space=pl.ANY)],
         out_specs=pl.BlockSpec(memory_space=pltpu.VMEM),
         scratch_shapes=[
+            pltpu.VMEM((lats * lons, rows, width), jnp.bfloat16),
             pltpu.VMEM((zs, rows, width), jnp.float32),
             pltpu.VMEM((zs, rows, width), jnp.float32),
             pltpu.VMEM((zs - 1, rows, width), jnp.float32),
-            pltpu.VMEM((HIGH_BLOCKS * LANES, 2 * TILE), jnp.bfloat16),
+            pltpu.VMEM((HIGH_BLOCKS * LANES, 2 * TILE), ONE_HOT),
             dma(()),
             dma((zs,)), dma((zs,)), dma((zs - 1,)), dma((zs - 1,)),
             dma((sends,)), dma((lats * lons,)),
@@ -238,8 +260,7 @@
 
 def body(lats, lons, transport, sigma_class, basin_id, depth_levels):
     table = bin_rows(transport, sigma_class, basin_id, depth_levels)
-    whole = share_rows(lats, lons, table).reshape(-1, BASINS, TILE)
-    return jnp.transpose(whole[:, :, :CLASSES], (1, 2, 0))
+    return share_rows(lats, lons, table)
 
 
 def solution(mesh):

time: 86.3 us -> 70.5 us (0.82)
  Pallas kernels: 82.8 us -> 68 us
  local copies, waits for them, and re-layouts: 3.27 us -> 2.09 us
    pallas_call x1, Pallas kernels: 55.1 us -> 40.7 us  [bin_rows(): pl.pallas_call(bin_kernel, grid=(row_count // STEP_ROWS,), in_specs=[deep...]
    reshape x1 -> x0, local copies, waits for them, and re-layouts: 1.86 us -> none  [body(): whole = share_rows(lats, lons, table).reshape(-1, BASINS, TILE)]
where the time goes in v1:
time: 70.5 us; the launch traced here: 70.1 us
  Pallas kernels  68 us (96%)
  local copies, waits for them, and re-layouts  2.09 us (3%)
    pallas_call x1, Pallas kernels, bin_rows(): pl.pallas_call(bin_kernel, grid=(row_count // STEP_ROWS,), in_specs=[deep...  40.7 us
    pallas_call x1, Pallas kernels, share_rows(): pl.pallas_call(functools.partial(share_kernel, lats, lons), out_shape=jax...  27.3 us
    unnamed x1, local copies, waits for them, and re-layouts  2.09 us

profile of v1, /device:TPU:0, one launch (start us, length us, event | category | flops | bytes accessed | tf_op | source)
XLA Modules:
  0.0 70.1 jit_solution(9167304256441480890)
XLA Ops:
  0.0 40.7 %bin_rows.1 = f32[128,1024]{1,0:T(8,128)} custom-call(bf16[48,128,384]{2,1,0:T(8,128)(2,1)} %refs_0_.1, s32[48,128,384]{2,1,0:T(8,128)} %refs_1_.1, s32[128,384]{1,0:T(8,128)} %refs_2_.1, s32[128,384]{1,0:T(8,128)} %refs_3_.1), custom_call_target="tpu_custom_call" | custom-call | tf_op jit(solution)/shard_map/bin_rows/pallas_call | solution.py:100
  40.7 27.3 %share_rows.1 = bf16[4,200,512]{2,1,0:T(8,128)(2,1)} custom-call(f32[8,16,1024]{2,1,0:T(8,128)} %bitcast.1, f8e4m3fn[512,512]{1,0:T(32,128)(4,1)} %constant.2.clone.sums_ref), custom_call_target="tpu_custom_call" | custom-call | tf_op jit(solution)/shard_map/share_rows/pallas_call | solution.py:241
  68.0 2.1 %copy.7 = bf16[4,200,512]{2,1,0:T(8,128)(2,1)} copy(bf16[4,200,512]{2,1,0:T(8,128)(2,1)} %share_rows.1) | data formatting | bytes 1638400

commit v2 on v1

v2 whole, which is shorter than its diff:
```python
import functools

import jax
import jax.numpy as jnp
import numpy as np
from jax import lax
from jax.experimental import pallas as pl
from jax.experimental.pallas import tpu as pltpu
from jax.sharding import PartitionSpec as P

CLASSES = 200
BASINS = 4
SUB = 8
LANES = 128
TILE = 256
UNIT = 16
MESH = pl.DeviceIdType.MESH
HIGHS = 26
HIGH_BLOCKS = 4
ONE_HOT = jnp.float8_e4m3fn


def high_rows(high, value):
    pair = jnp.concatenate([high, high - 1], axis=0).astype(jnp.int16)
    zero = jnp.bfloat16(0)
    return jnp.concatenate([jnp.where(pair == jnp.int16(i), value, zero) for i in range(0, HIGHS, 2)], axis=0)


def low_rows(low):
    four = jnp.concatenate([low - i for i in range(4)], axis=0).astype(jnp.int8)
    one, zero = ONE_HOT(1), ONE_HOT(0)
    return jnp.concatenate([jnp.where(four == jnp.int8(i), one, zero) for i in range(0, TILE // SUB, 4)], axis=0)


def squeeze_rows(product):
    rows = lax.broadcasted_iota(jnp.int32, (SUB, TILE), 0)
    lanes = lax.broadcasted_iota(jnp.int32, (SUB, TILE), 1)
    own = (lanes % SUB) == rows
    blocks = []
    for q in range(HIGH_BLOCKS):
        total = None
        for s in range(SUB):
            high = q * SUB + s
            if high * SUB >= CLASSES:
                break
            piece = jnp.where(own, product[high * SUB:(high + 1) * SUB, :], 0.0)
            piece = piece if s == 0 else pltpu.roll(piece, s, 1)
            total = piece if total is None else total + piece
        straight = jnp.where(rows == 0, total, 0.0)
        for r in range(1, SUB):
            straight = jnp.where(rows == r, pltpu.roll(total, TILE - r, 1), straight)
        blocks.append(straight)
    return jnp.concatenate(blocks, axis=1)


def running_sums():
    row = np.arange(HIGH_BLOCKS * LANES)
    column = np.arange(2 * TILE)
    lane = row % LANES
    klass = (row // LANES) * 64 + (lane % SUB) * SUB + (lane % 64) // SUB
    same = (lane // 64)[:, None] == (column // TILE)[None, :]
    return (same & (klass[:, None] <= (column % TILE)[None, :])).astype(ONE_HOT)


def accumulate(share, sums, acc0, acc1):
    parts = []
    for pair in range(BASINS // 2):
        lanes = [share[:, q * TILE + pair * LANES:q * TILE + (pair + 1) * LANES] for q in range(HIGH_BLOCKS)]
        rest = jnp.concatenate(lanes, axis=1)
        for _ in range(3):
            part = rest.astype(jnp.bfloat16).astype(jnp.float32)
            rest = rest - part
            parts.append(part)
    left = jnp.concatenate(parts, axis=0).astype(jnp.bfloat16)
    rows = share.shape[0]
    for k in range(2):
        for n, acc in enumerate((acc0, acc1)):
            right = sums[k * TILE:(k + 1) * TILE, n * TILE:(n + 1) * TILE]
            pltpu.matmul_push_rhs(right, staging_register=k, mxu_index=n)
            pltpu.matmul_acc_lhs(acc, left[:, k * TILE:(k + 1) * TILE], load_staged_rhs=k)
    pieces = []
    halves = [pltpu.matmul_pop(acc0), pltpu.matmul_pop(acc1)]
    for pair in range(BASINS // 2):
        for total in halves:
            three = [total[(pair * 3 + i) * rows:(pair * 3 + i + 1) * rows] for i in range(3)]
            pieces.append(three[0] + three[1] + three[2])
    return jnp.concatenate(pieces, axis=1)


def bin_half(flow_ref, class_ref, basin_ref, depth_ref, half, accs):
    levels, _, cols = class_ref.shape
    rows = slice(half * SUB, (half + 1) * SUB)
    depth = depth_ref[rows, :]
    base = basin_ref[rows, :] * SUB
    lefts, rights = [], []
    count = 0
    for level in range(levels):
        klass = class_ref[level, rows, :]
        flow = flow_ref[level].astype(jnp.float32)[rows]
        flow = jnp.where(level < depth, flow, 0.0)
        value = jnp.concatenate([flow, flow], axis=0).astype(jnp.bfloat16)
        left = high_rows(klass >> 3, value)
        right = low_rows(base + (klass & 7))
        for lane in range(0, cols, LANES):
            lefts.append(left[:, lane:lane + LANES])
            rights.append(right[:, lane:lane + LANES])
            if len(lefts) == 2:
                mxu, stage = count % 2, (count // 2) % 2
                count += 1
                pltpu.matmul_push_rhs(
                    jnp.concatenate(rights, axis=1), staging_register=stage, mxu_index=mxu, transpose=True)
                pltpu.matmul_acc_lhs(accs[mxu], jnp.concatenate(lefts, axis=1), load_staged_rhs=stage)
                lefts, rights = [], []


def drain(accs):
    return squeeze_rows(pltpu.matmul_pop(accs[0]) + pltpu.matmul_pop(accs[1]))


def fused_body(lats, lons, flow_ref, class_ref, basin_ref, depth_ref, sums_ref, out_ref,
               flows, classes, basins, depths, sums, table, half, acc, arrived, in_sems, misc_sems,
               half_send, half_recv, arr_send, arr_recv, out_send, own_send, fwd_send, out_recv,
               a0, a1, b0, b1, c0, c1):
    lat, lon = lax.axis_index("lat"), lax.axis_index("lon")
    zs = lons // 2
    z, core = lon // 2, lax.rem(lon, 2)
    units = classes.shape[0]
    partner = (lat, z * 2 + (1 - core))
    z_peers = [(lat, lax.rem(z + k, zs) * 2 + core) for k in range(1, zs)]
    lat_peers = [(lax.rem(lat + k, lats), lon) for k in range(1, lats)]

    def fetch(u):
        rows = pl.ds(pl.multiple_of(u * UNIT, UNIT), UNIT)
        return [
            pltpu.make_async_copy(flow_ref.at[:, rows, :], flows.at[u], in_sems.at[0, u]),
            pltpu.make_async_copy(class_ref.at[:, rows, :], classes.at[u], in_sems.at[1, u]),
            pltpu.make_async_copy(basin_ref.at[rows, :], basins.at[u], in_sems.at[2, u]),
            pltpu.make_async_copy(depth_ref.at[rows, :], depths.at[u], in_sems.at[3, u]),
        ]

    for u in range(units):
        for copy in fetch(u):
            copy.start()
    load = pltpu.make_async_copy(sums_ref, sums, misc_sems.at[0])
    load.start()
    barrier = pltpu.get_barrier_semaphore()
    everyone = [partner] + z_peers + lat_peers
    for peer in everyone:
        pl.semaphore_signal(barrier, inc=1, device_id=peer, device_id_type=MESH)
    pl.semaphore_wait(barrier, len(everyone))
    load.wait()

    def remote(src, dst, send_sem, recv_sem, peer):
        return pltpu.make_async_remote_copy(
            src_ref=src, dst_ref=dst, send_sem=send_sem, recv_sem=recv_sem,
            device_id=peer, device_id_type=MESH,
        )

    def owner_lon(u):
        return lax.rem(u + lons // 2, lons)

    def swap_copy(u):
        return remote(table.at[u + 1], half.at[u], half_send.at[u], half_recv.at[u], partner)

    def move_copy(u, k):
        return remote(acc.at[u], arrived.at[u, k - 1], arr_send.at[u], arr_recv.at[u, k - 1], z_peers[k - 1])

    def block_at(group, u):
        return out_ref.at[group * units + u]

    def block_copy(group, u, send_sem, peer):
        ref = block_at(group, u)
        return remote(ref, ref, send_sem, out_recv.at[group * units + u], peer)

    def landed(group, u):
        block_copy(group, u, own_send.at[0, 0], partner).wait_recv()

    def swap(u):
        @pl.when(lax.rem(owner_lon(u), 2) != core)
        def _():
            swap_copy(u).start()

    def merge(u):
        target = owner_lon(u)

        @pl.when(lax.rem(target, 2) == core)
        def _():
            swap_copy(u).wait_recv()
            acc[u] = table[u + 1].reshape(UNIT, -1) + half[u].reshape(UNIT, -1)
            for k in range(1, zs):
                @pl.when(target // 2 == lax.rem(z + k, zs))
                def _(k=k):
                    move_copy(u, k).start()

    def own_peers():
        return z_peers + lat_peers + [partner]

    def finish(u):
        @pl.when(owner_lon(u) == lon)
        def _():
            for k in range(1, zs):
                move_copy(u, k).wait_recv()
            share = acc[u]
            for k in range(1, zs):
                share = share + arrived[u, k - 1]
            out_ref[lat * units + u] = accumulate(share, sums[...], c0, c1).astype(jnp.bfloat16)
            for n, peer in enumerate(own_peers()):
                block_copy(lat, u, own_send.at[u, n], peer).start()

    def forward(u):
        target = owner_lon(u)

        @pl.when((lax.rem(target, 2) == core) & (target != lon))
        def _():
            landed(lat, u)
            for n, peer in enumerate(lat_peers + [partner]):
                block_copy(lat, u, own_send.at[u, n], peer).start()

    def relay(u):
        @pl.when(lax.rem(owner_lon(u), 2) == core)
        def _():
            for k in range(1, lats):
                group = lax.rem(lat - k + lats, lats)
                landed(group, u)
                block_copy(group, u, fwd_send.at[u, k - 1], partner).start()

    def when_unit(u, stage):
        @pl.when((u >= 0) & (u < units))
        def _():
            stage(u)

    def step(t, carry):
        for copy in fetch(t):
            copy.wait()
        refs = [flows.at[t], classes.at[t], basins.at[t], depths.at[t]]
        table[t, 1] = drain((b0, b1))
        bin_half(*refs, 0, (a0, a1))
        when_unit(t - 1, swap)
        table[t + 1, 0] = drain((a0, a1))
        bin_half(*refs, 1, (b0, b1))
        when_unit(t - 1, merge)
        when_unit(t - 2, finish)
        when_unit(t - 3, forward)
        when_unit(t - 4, relay)
        return carry

    lax.fori_loop(0, units, step, 0)
    table[units, 1] = drain((b0, b1))
    last = units - 1
    swap(last)
    for stage, u in ((finish, last - 1), (merge, last), (forward, last - 2), (relay, last - 3),
                     (finish, last), (forward, last - 1), (relay, last - 2), (forward, last),
                     (relay, last - 1), (relay, last)):
        if u >= 0:
            stage(u)

    def settle(u, carry):
        target = owner_lon(u)

        @pl.when(lax.rem(target, 2) != core)
        def _():
            swap_copy(u).wait_send()
            for group in range(lats):
                landed(group, u)

        @pl.when(lax.rem(target, 2) == core)
        def _():
            for k in range(1, lats):
                block_copy(lat, u, fwd_send.at[u, k - 1], partner).wait_send()

            @pl.when(target == lon)
            def _():
                for n, peer in enumerate(own_peers()):
                    block_copy(lat, u, own_send.at[u, n], peer).wait_send()

            @pl.when(target != lon)
            def _():
                move_copy(u, 1).wait_send()
                for n, peer in enumerate(lat_peers + [partner]):
                    block_copy(lat, u, own_send.at[u, n], peer).wait_send()
        return carry

    lax.fori_loop(0, units, settle, 0)


def fused_kernel(lats, lons, *refs):
    shape = (HIGHS * SUB, TILE)
    tail = (6 * UNIT, TILE)
    pl.run_scoped(
        functools.partial(fused_body, lats, lons, *refs),
        *[pltpu.ACC(m)(s, jnp.float32) for s in (shape, shape, tail) for m in (0, 1)],
    )


def fused(lats, lons, transport, sigma_class, basin_id, depth_levels):
    levels, row_count, cols = sigma_class.shape
    units = row_count // UNIT
    zs = lons // 2
    width = HIGH_BLOCKS * TILE
    dma = pltpu.SemaphoreType.DMA
    hbm = pl.BlockSpec(memory_space=pl.ANY)
    return pl.pallas_call(
        functools.partial(fused_kernel, lats, lons),
        out_shape=jax.ShapeDtypeStruct((lats * units, UNIT, width), jnp.bfloat16),
        in_specs=[hbm] * 5,
        out_specs=pl.BlockSpec(memory_space=pltpu.VMEM),
        scratch_shapes=[
            pltpu.VMEM((units, levels, UNIT, cols), jnp.bfloat16),
            pltpu.VMEM((units, levels, UNIT, cols), jnp.int32),
            pltpu.VMEM((units, UNIT, cols), jnp.int32),
            pltpu.VMEM((units, UNIT, cols), jnp.int32),
            pltpu.VMEM((HIGH_BLOCKS * LANES, 2 * TILE), ONE_HOT),
            pltpu.VMEM((units + 1, 2, SUB, width), jnp.float32),
            pltpu.VMEM((units, 2, SUB, width), jnp.float32),
            pltpu.VMEM((units, UNIT, width), jnp.float32),
            pltpu.VMEM((units, zs - 1, UNIT, width), jnp.float32),
            dma((4, units)), dma((1,)),
            dma((units,)), dma((units,)), dma((units,)), dma((units, zs - 1)),
            dma((1,)), dma((units, zs - 1 + lats)), dma((units, lats - 1)), dma((lats * units,)),
        ],
        compiler_params=pltpu.CompilerParams(collective_id=0, has_side_effects=True),
        name="fused_rows",
    )(transport, sigma_class, basin_id, depth_levels, jnp.asarray(running_sums()))


def turn_kernel(in_ref, out_ref):
    for basin in range(BASINS):
        block = in_ref[:, :, basin * TILE:(basin + 1) * TILE]
        turned = jnp.transpose(block.reshape(-1, TILE))
        out_ref[basin] = turned[:CLASSES]


def turn(whole):
    blocks, rows, width = whole.shape
    per = LANES // rows
    return pl.pallas_call(
        turn_kernel,
        grid=(blocks // per,),
        in_specs=[pl.BlockSpec((per, rows, width), lambda i: (i, 0, 0))],
        out_specs=pl.BlockSpec((BASINS, CLASSES, LANES), lambda i: (0, 0, i)),
        out_shape=jax.ShapeDtypeStruct((BASINS, CLASSES, blocks * rows), jnp.bfloat16),
        name="turn_rows",
    )(whole)


def body(lats, lons, transport, sigma_class, basin_id, depth_levels):
    return turn(fused(lats, lons, transport, sigma_class, basin_id, depth_levels))


def solution(mesh):
    placed = (P(None, "lat", "lon"), P(None, "lat", "lon"), P("lat", "lon"), P("lat", "lon"))
    local = functools.partial(body, mesh.shape["lat"], mesh.shape["lon"])
    return jax.shard_map(local, mesh=mesh, in_specs=placed, out_specs=P(), check_vma=False)
```

time: 70.5 us -> 60.5 us (0.86)
  Pallas kernels: 68 us -> 60.4 us
  local copies, waits for them, and re-layouts: 2.09 us -> 0 us
    pallas_call x2, Pallas kernels: 68 us -> 60.4 us  [the longest x1 56.8 us: fused(): pl.pallas_call(functools.partial(fused_kernel, lats, lons), out_shape=jax...]
    unnamed x1 -> x0, local copies, waits for them, and re-layouts: 2.09 us -> none
where the time goes in v2:
time: 60.5 us; the launch traced here: 60.4 us
  Pallas kernels  60.4 us (100%)
    pallas_call x1, Pallas kernels, fused(): pl.pallas_call(functools.partial(fused_kernel, lats, lons), out_shape=jax...  56.8 us
    pallas_call x1, Pallas kernels, turn(): pl.pallas_call(turn_kernel, grid=(blocks // per,), in_specs=[pl.BlockSpec...  3.52 us

profile of v2, /device:TPU:0, one launch (start us, length us, event | category | flops | bytes accessed | tf_op | source)
XLA Modules:
  0.0 60.4 jit_solution(8648383837968533)
XLA Ops:
  0.0 56.8 %fused_rows.1.in_ref = bf16[32,16,1024]{2,1,0:T(8,128)(2,1)} custom-call(bf16[48,128,384]{2,1,0:T(8,128)(2,1)} %refs_0_.1, s32[48,128,384]{2,1,0:T(8,128)} %refs_1_.1, s32[128,384]{1,0:T(8,128)} %refs_2_.1, s32[128,384]{1,0:T(8,128)} %refs_3_.1, f8e4m3fn[512,512]{1,0:T(32,128)(4,1)} %constant.2.clone.refs_4_), custom_call_target="tpu_custom_call" | custom-call | tf_op jit(solution)/shard_map/fused_rows/pallas_call | solution.py:302
  56.8 3.5 %turn_rows.1 = bf16[4,200,512]{2,1,0:T(8,128)(2,1)} custom-call(bf16[32,16,1024]{2,1,0:T(8,128)(2,1)} %fused_rows.1.in_ref), custom_call_target="tpu_custom_call" | custom-call | tf_op jit(solution)/shard_map/turn_rows/pallas_call | solution.py:336

commit v3 on v2

--- a/solution.py
+++ b/solution.py
@@ -118,8 +118,8 @@
 
 
 def fused_body(lats, lons, flow_ref, class_ref, basin_ref, depth_ref, sums_ref, out_ref,
-               flows, classes, basins, depths, sums, table, half, acc, arrived, in_sems, misc_sems,
-               half_send, half_recv, arr_send, arr_recv, out_send, own_send, fwd_send, out_recv,
+               flows, classes, basins, depths, sums, table, half, acc, arrived, mine, in_sems, misc_sems,
+               half_send, half_recv, arr_send, arr_recv, own_sem, own_send, fwd_send, out_recv,
                a0, a1, b0, b1, c0, c1):
     lat, lon = lax.axis_index("lat"), lax.axis_index("lon")
     zs = lons // 2
@@ -172,6 +172,12 @@
         ref = block_at(group, u)
         return remote(ref, ref, send_sem, out_recv.at[group * units + u], peer)
 
+    def own_copy(u, n, peer):
+        return remote(mine.at[u], block_at(lat, u), own_send.at[u, n], out_recv.at[lat * units + u], peer)
+
+    def keep_copy(u):
+        return pltpu.make_async_copy(mine.at[u], block_at(lat, u), own_sem.at[u])
+
     def landed(group, u):
         block_copy(group, u, own_send.at[0, 0], partner).wait_recv()
 
@@ -203,9 +209,10 @@
             share = acc[u]
             for k in range(1, zs):
                 share = share + arrived[u, k - 1]
-            out_ref[lat * units + u] = accumulate(share, sums[...], c0, c1).astype(jnp.bfloat16)
+            mine[u] = accumulate(share, sums[...], c0, c1).astype(jnp.bfloat16)
             for n, peer in enumerate(own_peers()):
-                block_copy(lat, u, own_send.at[u, n], peer).start()
+                own_copy(u, n, peer).start()
+            keep_copy(u).start()
 
     def forward(u):
         target = owner_lon(u)
@@ -271,7 +278,8 @@
             @pl.when(target == lon)
             def _():
                 for n, peer in enumerate(own_peers()):
-                    block_copy(lat, u, own_send.at[u, n], peer).wait_send()
+                    own_copy(u, n, peer).wait_send()
+                keep_copy(u).wait()
 
             @pl.when(target != lon)
             def _():
@@ -298,12 +306,13 @@
     zs = lons // 2
     width = HIGH_BLOCKS * TILE
     dma = pltpu.SemaphoreType.DMA
-    hbm = pl.BlockSpec(memory_space=pl.ANY)
+    hbm = pl.BlockSpec(memory_space=pltpu.HBM)
+    operands = (transport, sigma_class, basin_id, depth_levels, jnp.asarray(running_sums()))
     return pl.pallas_call(
         functools.partial(fused_kernel, lats, lons),
         out_shape=jax.ShapeDtypeStruct((lats * units, UNIT, width), jnp.bfloat16),
         in_specs=[hbm] * 5,
-        out_specs=pl.BlockSpec(memory_space=pltpu.VMEM),
+        out_specs=pl.BlockSpec(memory_space=pl.ANY),
         scratch_shapes=[
             pltpu.VMEM((units, levels, UNIT, cols), jnp.bfloat16),
             pltpu.VMEM((units, levels, UNIT, cols), jnp.int32),
@@ -314,31 +323,40 @@
             pltpu.VMEM((units, 2, SUB, width), jnp.float32),
             pltpu.VMEM((units, UNIT, width), jnp.float32),
             pltpu.VMEM((units, zs - 1, UNIT, width), jnp.float32),
+            pltpu.VMEM((units, UNIT, width), jnp.bfloat16),
             dma((4, units)), dma((1,)),
             dma((units,)), dma((units,)), dma((units,)), dma((units, zs - 1)),
-            dma((1,)), dma((units, zs - 1 + lats)), dma((units, lats - 1)), dma((lats * units,)),
+            dma((units,)), dma((units, zs - 1 + lats)), dma((units, lats - 1)), dma((lats * units,)),
         ],
-        compiler_params=pltpu.CompilerParams(collective_id=0, has_side_effects=True),
+        compiler_params=pltpu.CompilerParams(
+            collective_id=0, has_side_effects=True, vmem_limit_bytes=40 * 1024 * 1024),
         name="fused_rows",
-    )(transport, sigma_class, basin_id, depth_levels, jnp.asarray(running_sums()))
-
-
-def turn_kernel(in_ref, out_ref):
+    )(*[pltpu.with_memory_space_constraint(x, pltpu.HBM) for x in operands])
+
+
+def turn_kernel(in_ref, out_ref, turned, sems):
+    blocks, rows, _ = in_ref.shape
+    copies = []
     for basin in range(BASINS):
-        block = in_ref[:, :, basin * TILE:(basin + 1) * TILE]
-        turned = jnp.transpose(block.reshape(-1, TILE))
-        out_ref[basin] = turned[:CLASSES]
+        for lane in range(0, blocks * rows, LANES):
+            block = in_ref[lane // rows:(lane + LANES) // rows, :, basin * TILE:(basin + 1) * TILE]
+            turned[basin, :, lane:lane + LANES] = jnp.transpose(block.reshape(LANES, TILE))[:CLASSES]
+        copies.append(pltpu.make_async_copy(turned.at[basin], out_ref.at[basin], sems.at[basin]))
+        copies[-1].start()
+    for copy in copies:
+        copy.wait()
 
 
 def turn(whole):
     blocks, rows, width = whole.shape
-    per = LANES // rows
+    shape = (BASINS, CLASSES, blocks * rows)
     return pl.pallas_call(
         turn_kernel,
-        grid=(blocks // per,),
-        in_specs=[pl.BlockSpec((per, rows, width), lambda i: (i, 0, 0))],
-        out_specs=pl.BlockSpec((BASINS, CLASSES, LANES), lambda i: (0, 0, i)),
-        out_shape=jax.ShapeDtypeStruct((BASINS, CLASSES, blocks * rows), jnp.bfloat16),
+        in_specs=[pl.BlockSpec(memory_space=pltpu.VMEM)],
+        out_specs=pl.BlockSpec(memory_space=pl.ANY),
+        out_shape=jax.ShapeDtypeStruct(shape, jnp.bfloat16),
+        scratch_shapes=[pltpu.VMEM(shape, jnp.bfloat16), pltpu.SemaphoreType.DMA((BASINS,))],
+        compiler_params=pltpu.CompilerParams(vmem_limit_bytes=16 * 1024 * 1024),
         name="turn_rows",
     )(whole)
 

time: 60.5 us -> 57.2 us (0.945)
  Pallas kernels: 60.4 us -> 57 us
    pallas_call x1, Pallas kernels: 3.52 us -> 1.04 us  [turn(): pl.pallas_call(turn_kernel, in_specs=[pl.BlockSpec(memory_space=pltpu.VME...]
    pallas_call x1, Pallas kernels: 56.8 us -> 56 us  [fused(): pl.pallas_call(functools.partial(fused_kernel, lats, lons), out_shape=jax...]
where the time goes in v3:
time: 57.2 us; the launch traced here: 57 us
  Pallas kernels  57 us (100%)
    pallas_call x1, Pallas kernels, fused(): pl.pallas_call(functools.partial(fused_kernel, lats, lons), out_shape=jax...  56 us

profile of v3, /device:TPU:0, one launch (start us, length us, event | category | flops | bytes accessed | tf_op | source)
XLA Modules:
  0.0 57.0 jit_solution(5499183241524817047)
XLA Ops:
  0.0 56.0 %fused_rows.1.in_ref = bf16[32,16,1024]{2,1,0:T(8,128)(2,1)S(1)} custom-call(bf16[48,128,384]{2,1,0:T(8,128)(2,1)} %refs_0_.1, s32[48,128,384]{2,1,0:T(8,128)} %refs_1_.1, s32[128,384]{1,0:T(8,128)} %refs_2_.1, s32[128,384]{1,0:T(8,128)} %refs_3_.1, f8e4m3fn[512,512]{1,0:T(32,128)(4,1)} %constant.2.clone.refs_4_), custom_call_target="tpu_custom_call" | custom-call | tf_op jit(solution)/shard_map/fused_rows/pallas_call | solution.py:311
  56.0 1.0 %turn_rows.1 = bf16[4,200,512]{2,1,0:T(8,128)(2,1)} custom-call(bf16[32,16,1024]{2,1,0:T(8,128)(2,1)S(1)} %fused_rows.1.in_ref), custom_call_target="tpu_custom_call" | custom-call | tf_op jit(solution)/shard_map/turn_rows/pallas_call | solution.py:353

commit v4 on v3

v4 whole, which is shorter than its diff:
```python
import functools

import jax
import jax.numpy as jnp
import numpy as np
from jax import lax
from jax.experimental import pallas as pl
from jax.experimental.pallas import tpu as pltpu
from jax.sharding import PartitionSpec as P

CLASSES = 200
BASINS = 4
SUB = 8
LANES = 128
TILE = 256
UNIT = 16
MESH = pl.DeviceIdType.MESH
HIGHS = 26
HIGH_BLOCKS = 4
ONE_HOT = jnp.float8_e4m3fn


def high_rows(high, value):
    pair = jnp.concatenate([high, high - 1], axis=0).astype(jnp.int16)
    zero = jnp.bfloat16(0)
    return jnp.concatenate([jnp.where(pair == jnp.int16(i), value, zero) for i in range(0, HIGHS, 2)], axis=0)


def low_rows(low):
    four = jnp.concatenate([low - i for i in range(4)], axis=0).astype(jnp.int8)
    one, zero = ONE_HOT(1), ONE_HOT(0)
    return jnp.concatenate([jnp.where(four == jnp.int8(i), one, zero) for i in range(0, TILE // SUB, 4)], axis=0)


def squeeze_rows(product):
    rows = lax.broadcasted_iota(jnp.int32, (SUB, TILE), 0)
    lanes = lax.broadcasted_iota(jnp.int32, (SUB, TILE), 1)
    own = (lanes % SUB) == rows
    blocks = []
    for q in range(HIGH_BLOCKS):
        total = None
        for s in range(SUB):
            high = q * SUB + s
            if high * SUB >= CLASSES:
                break
            piece = jnp.where(own, product[high * SUB:(high + 1) * SUB, :], 0.0)
            piece = piece if s == 0 else pltpu.roll(piece, s, 1)
            total = piece if total is None else total + piece
        straight = jnp.where(rows == 0, total, 0.0)
        for r in range(1, SUB):
            straight = jnp.where(rows == r, pltpu.roll(total, TILE - r, 1), straight)
        blocks.append(straight)
    return jnp.concatenate(blocks, axis=1)


def running_sums():
    row = np.arange(HIGH_BLOCKS * LANES)
    column = np.arange(2 * TILE)
    lane = row % LANES
    klass = (row // LANES) * 64 + (lane % SUB) * SUB + (lane % 64) // SUB
    same = (lane // 64)[:, None] == (column // TILE)[None, :]
    return (same & (klass[:, None] <= (column % TILE)[None, :])).astype(ONE_HOT)


def accumulate(share, sums, acc0, acc1):
    parts = []
    for pair in range(BASINS // 2):
        lanes = [share[:, q * TILE + pair * LANES:q * TILE + (pair + 1) * LANES] for q in range(HIGH_BLOCKS)]
        rest = jnp.concatenate(lanes, axis=1)
        for _ in range(3):
            part = rest.astype(jnp.bfloat16).astype(jnp.float32)
            rest = rest - part
            parts.append(part)
    left = jnp.concatenate(parts, axis=0).astype(jnp.bfloat16)
    rows = share.shape[0]
    for k in range(2):
        for n, acc in enumerate((acc0, acc1)):
            right = sums[k * TILE:(k + 1) * TILE, n * TILE:(n + 1) * TILE]
            pltpu.matmul_push_rhs(right, staging_register=k, mxu_index=n)
            pltpu.matmul_acc_lhs(acc, left[:, k * TILE:(k + 1) * TILE], load_staged_rhs=k)
    pieces = []
    halves = [pltpu.matmul_pop(acc0), pltpu.matmul_pop(acc1)]
    for pair in range(BASINS // 2):
        for total in halves:
            three = [total[(pair * 3 + i) * rows:(pair * 3 + i + 1) * rows] for i in range(3)]
            pieces.append(three[0] + three[1] + three[2])
    return jnp.concatenate(pieces, axis=1)


def bin_half(flow_ref, class_ref, basin_ref, depth_ref, half, accs):
    levels, _, cols = class_ref.shape
    rows = slice(half * SUB, (half + 1) * SUB)
    depth = depth_ref[rows, :]
    base = basin_ref[rows, :] * SUB
    lefts, rights = [], []
    count = 0
    for level in range(levels):
        klass = class_ref[level, rows, :]
        flow = flow_ref[level].astype(jnp.float32)[rows]
        flow = jnp.where(level < depth, flow, 0.0)
        value = jnp.concatenate([flow, flow], axis=0).astype(jnp.bfloat16)
        left = high_rows(klass >> 3, value)
        right = low_rows(base + (klass & 7))
        for lane in range(0, cols, LANES):
            lefts.append(left[:, lane:lane + LANES])
            rights.append(right[:, lane:lane + LANES])
            if len(lefts) == 2:
                mxu, stage = count % 2, (count // 2) % 2
                count += 1
                pltpu.matmul_push_rhs(
                    jnp.concatenate(rights, axis=1), staging_register=stage, mxu_index=mxu, transpose=True)
                pltpu.matmul_acc_lhs(accs[mxu], jnp.concatenate(lefts, axis=1), load_staged_rhs=stage)
                lefts, rights = [], []


def drain(accs):
    return squeeze_rows(pltpu.matmul_pop(accs[0]) + pltpu.matmul_pop(accs[1]))


def fused_body(lats, lons, flow_ref, class_ref, basin_ref, depth_ref, sums_ref, out_ref,
               flows, classes, basins, depths, sums, table, arrived, mine, in_sems, sum_sem,
               move_send, move_recv, keep_sem, own_send, lat_send, out_recv, a0, a1, b0, b1, c0, c1):
    lat, lon = lax.axis_index("lat"), lax.axis_index("lon")
    steps = classes.shape[0]
    units = steps * (UNIT // SUB)
    column = [(lat, lax.rem(lon + k, lons)) for k in range(1, lons)]
    lat_peers = [(lax.rem(lat + k, lats), lon) for k in range(1, lats)]

    def fetch(t):
        rows = pl.ds(pl.multiple_of(t * UNIT, UNIT), UNIT)
        return [
            pltpu.make_async_copy(flow_ref.at[:, rows, :], flows.at[t], in_sems.at[0, t]),
            pltpu.make_async_copy(class_ref.at[:, rows, :], classes.at[t], in_sems.at[1, t]),
            pltpu.make_async_copy(basin_ref.at[rows, :], basins.at[t], in_sems.at[2, t]),
            pltpu.make_async_copy(depth_ref.at[rows, :], depths.at[t], in_sems.at[3, t]),
        ]

    for t in range(steps):
        for copy in fetch(t):
            copy.start()
    load = pltpu.make_async_copy(sums_ref, sums, sum_sem)
    load.start()
    barrier = pltpu.get_barrier_semaphore()
    for peer in column + lat_peers:
        pl.semaphore_signal(barrier, inc=1, device_id=peer, device_id_type=MESH)

    def remote(src, dst, send_sem, recv_sem, peer):
        return pltpu.make_async_remote_copy(
            src_ref=src, dst_ref=dst, send_sem=send_sem, recv_sem=recv_sem,
            device_id=peer, device_id_type=MESH,
        )

    def owner(u):
        return lax.rem(u + lons // 2, lons)

    def move_copy(u, k):
        return remote(table.at[u + 1], arrived.at[u, k - 1], move_send.at[u], move_recv.at[u, k - 1], (lat, owner(u)))

    def block_copy(group, u, n, peer):
        ref = out_ref.at[group * units + u]
        return remote(ref, ref, lat_send.at[u, n], out_recv.at[group * units + u], peer)

    def own_copy(u, send_sem, peer):
        return remote(mine.at[u], out_ref.at[lat * units + u], send_sem, out_recv.at[lat * units + u], peer)

    def keep_copy(u):
        return pltpu.make_async_copy(mine.at[u], out_ref.at[lat * units + u], keep_sem.at[u])

    def move(u):
        @pl.when(owner(u) != lon)
        def _():
            move_copy(u, lax.rem(lon - owner(u) + lons, lons)).start()

    def finish(u):
        @pl.when(owner(u) == lon)
        def _():
            for k in range(1, lons):
                move_copy(u, k).wait_recv()
            share = table[u + 1]
            for k in range(1, lons):
                share = share + arrived[u, k - 1]
            mine[u] = accumulate(share, sums[...], c0, c1).astype(jnp.bfloat16)
            for n, peer in enumerate(column):
                own_copy(u, own_send.at[u, n], peer).start()
            for n, peer in enumerate(lat_peers):
                own_copy(u, lat_send.at[u, n], peer).start()
            keep_copy(u).start()

    def forward(u):
        @pl.when(owner(u) != lon)
        def _():
            block_copy(lat, u, 0, column[0]).wait_recv()
            for n, peer in enumerate(lat_peers):
                block_copy(lat, u, n, peer).start()

    def slot(s):
        for stage, u in ((move, s - 1), (finish, s - 3), (forward, s - 5)):
            @pl.when(u >= 0)
            def _(stage=stage, u=u):
                stage(u)

    def step(t, carry):
        for copy in fetch(t):
            copy.wait()
        refs = [flows.at[t], classes.at[t], basins.at[t], depths.at[t]]
        table[2 * t] = drain((b0, b1))
        bin_half(*refs, 0, (a0, a1))

        @pl.when(t == 0)
        def _():
            pl.semaphore_wait(barrier, len(column) + len(lat_peers))
            load.wait()

        slot(2 * t)
        table[2 * t + 1] = drain((a0, a1))
        bin_half(*refs, 1, (b0, b1))
        slot(2 * t + 1)
        return carry

    lax.fori_loop(0, steps, step, 0)
    table[units] = drain((b0, b1))
    last = units - 1
    for stage, u in ((move, last), (finish, last - 2), (forward, last - 4), (finish, last - 1), (forward, last - 3),
                     (finish, last), (forward, last - 2), (forward, last - 1), (forward, last)):
        if u >= 0:
            stage(u)

    def settle(u, carry):
        for k in range(1, lats):
            block_copy(lax.rem(lat + k, lats), u, 0, column[0]).wait_recv()

        @pl.when(owner(u) == lon)
        def _():
            for n, peer in enumerate(column):
                own_copy(u, own_send.at[u, n], peer).wait_send()
            keep_copy(u).wait()

        @pl.when(owner(u) != lon)
        def _():
            move_copy(u, 1).wait_send()

        for n, peer in enumerate(lat_peers):
            block_copy(lat, u, n, peer).wait_send()
        return carry

    lax.fori_loop(0, units, settle, 0)


def fused_kernel(lats, lons, *refs):
    shape = (HIGHS * SUB, TILE)
    tail = (6 * SUB, TILE)
    pl.run_scoped(
        functools.partial(fused_body, lats, lons, *refs),
        *[pltpu.ACC(m)(s, jnp.float32) for s in (shape, shape, tail) for m in (0, 1)],
    )


def fused(lats, lons, transport, sigma_class, basin_id, depth_levels):
    levels, row_count, cols = sigma_class.shape
    steps = row_count // UNIT
    units = row_count // SUB
    width = HIGH_BLOCKS * TILE
    dma = pltpu.SemaphoreType.DMA
    hbm = pl.BlockSpec(memory_space=pltpu.HBM)
    operands = (transport, sigma_class, basin_id, depth_levels, jnp.asarray(running_sums()))
    return pl.pallas_call(
        functools.partial(fused_kernel, lats, lons),
        out_shape=jax.ShapeDtypeStruct((lats * units, SUB, width), jnp.bfloat16),
        in_specs=[hbm] * 5,
        out_specs=pl.BlockSpec(memory_space=pl.ANY),
        scratch_shapes=[
            pltpu.VMEM((steps, levels, UNIT, cols), jnp.bfloat16),
            pltpu.VMEM((steps, levels, UNIT, cols), jnp.int32),
            pltpu.VMEM((steps, UNIT, cols), jnp.int32),
            pltpu.VMEM((steps, UNIT, cols), jnp.int32),
            pltpu.VMEM((HIGH_BLOCKS * LANES, 2 * TILE), ONE_HOT),
            pltpu.VMEM((units + 1, SUB, width), jnp.float32),
            pltpu.VMEM((units, lons - 1, SUB, width), jnp.float32),
            pltpu.VMEM((units, SUB, width), jnp.bfloat16),
            dma((4, steps)), dma(()),
            dma((units,)), dma((units, lons - 1)), dma((units,)),
            dma((units, lons - 1)), dma((units, lats - 1)), dma((lats * units,)),
        ],
        compiler_params=pltpu.CompilerParams(
            collective_id=0, has_side_effects=True, vmem_limit_bytes=40 * 1024 * 1024),
        name="fused_rows",
    )(*[pltpu.with_memory_space_constraint(x, pltpu.HBM) for x in operands])


def turn_kernel(in_ref, out_ref, turned, sems):
    blocks, rows, _ = in_ref.shape
    copies = []
    for basin in range(BASINS):
        for lane in range(0, blocks * rows, LANES):
            block = in_ref[lane // rows:(lane + LANES) // rows, :, basin * TILE:(basin + 1) * TILE]
            turned[basin, :, lane:lane + LANES] = jnp.transpose(block.reshape(LANES, TILE))[:CLASSES]
        copies.append(pltpu.make_async_copy(turned.at[basin], out_ref.at[basin], sems.at[basin]))
        copies[-1].start()
    for copy in copies:
        copy.wait()


def turn(whole):
    blocks, rows, width = whole.shape
    shape = (BASINS, CLASSES, blocks * rows)
    return pl.pallas_call(
        turn_kernel,
        in_specs=[pl.BlockSpec(memory_space=pltpu.VMEM)],
        out_specs=pl.BlockSpec(memory_space=pl.ANY),
        out_shape=jax.ShapeDtypeStruct(shape, jnp.bfloat16),
        scratch_shapes=[pltpu.VMEM(shape, jnp.bfloat16), pltpu.SemaphoreType.DMA((BASINS,))],
        compiler_params=pltpu.CompilerParams(vmem_limit_bytes=16 * 1024 * 1024),
        name="turn_rows",
    )(whole)


def body(lats, lons, transport, sigma_class, basin_id, depth_levels):
    return turn(fused(lats, lons, transport, sigma_class, basin_id, depth_levels))


def solution(mesh):
    placed = (P(None, "lat", "lon"), P(None, "lat", "lon"), P("lat", "lon"), P("lat", "lon"))
    local = functools.partial(body, mesh.shape["lat"], mesh.shape["lon"])
    return jax.shard_map(local, mesh=mesh, in_specs=placed, out_specs=P(), check_vma=False)
```

time: 57.2 us -> 57.6 us (level)
  no operation moved by 1% of the time
where the time goes in v4:
time: 57.6 us; the launch traced here: 57.5 us
  Pallas kernels  57.5 us (100%)
    pallas_call x1, Pallas kernels, fused(): pl.pallas_call(functools.partial(fused_kernel, lats, lons), out_shape=jax...  56.4 us

profile of v4, /device:TPU:0, one launch (start us, length us, event | category | flops | bytes accessed | tf_op | source)
XLA Modules:
  0.0 57.5 jit_solution(5748837549756001922)
XLA Ops:
  0.0 56.4 %fused_rows.1.in_ref = bf16[64,8,1024]{2,1,0:T(8,128)(2,1)S(1)} custom-call(bf16[48,128,384]{2,1,0:T(8,128)(2,1)} %refs_0_.1, s32[48,128,384]{2,1,0:T(8,128)} %refs_1_.1, s32[128,384]{1,0:T(8,128)} %refs_2_.1, s32[128,384]{1,0:T(8,128)} %refs_3_.1, f8e4m3fn[512,512]{1,0:T(32,128)(4,1)} %constant.2.clone.refs_4_), custom_call_target="tpu_custom_call" | custom-call | tf_op jit(solution)/shard_map/fused_rows/pallas_call | solution.py:266
  56.4 1.0 %turn_rows.1 = bf16[4,200,512]{2,1,0:T(8,128)(2,1)} custom-call(bf16[64,8,1024]{2,1,0:T(8,128)(2,1)S(1)} %fused_rows.1.in_ref), custom_call_target="tpu_custom_call" | custom-call | tf_op jit(solution)/shard_map/turn_rows/pallas_call | solution.py:306

commit v5 on v4

--- a/solution.py
+++ b/solution.py
@@ -151,7 +151,11 @@
         )
 
     def owner(u):
-        return lax.rem(u + lons // 2, lons)
+        zs = lons // 2
+        back = lax.rem(2 * units - 1 - u, lons)
+        i = lax.rem(back, zs)
+        z = zs // 2 - 1 - i // 2 + lax.rem(i, 2) * (1 + 2 * (i // 2))
+        return 2 * z + lax.rem(1 + back + back // zs, 2)
 
     def move_copy(u, k):
         return remote(table.at[u + 1], arrived.at[u, k - 1], move_send.at[u], move_recv.at[u, k - 1], (lat, owner(u)))
@@ -193,31 +197,33 @@
             for n, peer in enumerate(lat_peers):
                 block_copy(lat, u, n, peer).start()
 
-    def slot(s):
-        for stage, u in ((move, s - 1), (finish, s - 3), (forward, s - 5)):
-            @pl.when(u >= 0)
-            def _(stage=stage, u=u):
-                stage(u)
-
-    def step(t, carry):
+    def from_zero(stage, u):
+        @pl.when(u >= 0)
+        def _():
+            stage(u)
+
+    def bin_unit_pair(t, between):
         for copy in fetch(t):
             copy.wait()
         refs = [flows.at[t], classes.at[t], basins.at[t], depths.at[t]]
         table[2 * t] = drain((b0, b1))
         bin_half(*refs, 0, (a0, a1))
-
-        @pl.when(t == 0)
-        def _():
-            pl.semaphore_wait(barrier, len(column) + len(lat_peers))
-            load.wait()
-
-        slot(2 * t)
+        between()
         table[2 * t + 1] = drain((a0, a1))
         bin_half(*refs, 1, (b0, b1))
-        slot(2 * t + 1)
+
+    def step(t, carry):
+        bin_unit_pair(t, lambda: move(2 * t - 1))
+        move(2 * t)
+        for stage, late in ((finish, 3), (finish, 2), (forward, 5), (forward, 4)):
+            from_zero(stage, 2 * t - late)
         return carry
 
-    lax.fori_loop(0, steps, step, 0)
+    bin_unit_pair(0, lambda: None)
+    pl.semaphore_wait(barrier, len(column) + len(lat_peers))
+    load.wait()
+    move(0)
+    lax.fori_loop(1, steps, step, 0)
     table[units] = drain((b0, b1))
     last = units - 1
     for stage, u in ((move, last), (finish, last - 2), (forward, last - 4), (finish, last - 1), (forward, last - 3),

time: 57.6 us -> 53.6 us (0.931)
  Pallas kernels: 57.5 us -> 53.5 us
    pallas_call x1, Pallas kernels: 56.4 us -> 52.4 us  [fused(): pl.pallas_call(functools.partial(fused_kernel, lats, lons), out_shape=jax...]
where the time goes in v5:
time: 53.6 us; the launch traced here: 53.5 us
  Pallas kernels  53.5 us (100%)
    pallas_call x1, Pallas kernels, fused(): pl.pallas_call(functools.partial(fused_kernel, lats, lons), out_shape=jax...  52.4 us

profile of v5, /device:TPU:0, one launch (start us, length us, event | category | flops | bytes accessed | tf_op | source)
XLA Modules:
  0.0 53.5 jit_solution(8303532955270459419)
XLA Ops:
  0.0 52.4 %fused_rows.1.in_ref = bf16[64,8,1024]{2,1,0:T(8,128)(2,1)S(1)} custom-call(bf16[48,128,384]{2,1,0:T(8,128)(2,1)} %refs_0_.1, s32[48,128,384]{2,1,0:T(8,128)} %refs_1_.1, s32[128,384]{1,0:T(8,128)} %refs_2_.1, s32[128,384]{1,0:T(8,128)} %refs_3_.1, f8e4m3fn[512,512]{1,0:T(32,128)(4,1)} %constant.2.clone.refs_4_), custom_call_target="tpu_custom_call" | custom-call | tf_op jit(solution)/shard_map/fused_rows/pallas_call | solution.py:272
  52.4 1.0 %turn_rows.1 = bf16[4,200,512]{2,1,0:T(8,128)(2,1)} custom-call(bf16[64,8,1024]{2,1,0:T(8,128)(2,1)S(1)} %fused_rows.1.in_ref), custom_call_target="tpu_custom_call" | custom-call | tf_op jit(solution)/shard_map/turn_rows/pallas_call | solution.py:312

commit v6 on v5

--- a/solution.py
+++ b/solution.py
@@ -14,6 +14,7 @@
 LANES = 128
 TILE = 256
 UNIT = 16
+STEP = 32
 MESH = pl.DeviceIdType.MESH
 HIGHS = 26
 HIGH_BLOCKS = 4
@@ -87,7 +88,7 @@
     return jnp.concatenate(pieces, axis=1)
 
 
-def bin_half(flow_ref, class_ref, basin_ref, depth_ref, half, accs):
+def bin_half(flow_ref, class_ref, basin_ref, depth_ref, half, accs, middle=None):
     levels, _, cols = class_ref.shape
     rows = slice(half * SUB, (half + 1) * SUB)
     depth = depth_ref[rows, :]
@@ -95,6 +96,8 @@
     lefts, rights = [], []
     count = 0
     for level in range(levels):
+        if level == levels // 2 and middle is not None:
+            middle()
         klass = class_ref[level, rows, :]
         flow = flow_ref[level].astype(jnp.float32)[rows]
         flow = jnp.where(level < depth, flow, 0.0)
@@ -202,34 +205,51 @@
         def _():
             stage(u)
 
-    def bin_unit_pair(t, between):
-        for copy in fetch(t):
-            copy.wait()
-        refs = [flows.at[t], classes.at[t], basins.at[t], depths.at[t]]
-        table[2 * t] = drain((b0, b1))
-        bin_half(*refs, 0, (a0, a1))
-        between()
-        table[2 * t + 1] = drain((a0, a1))
-        bin_half(*refs, 1, (b0, b1))
+    def bin_step(t, moves):
+        pairs = STEP // UNIT
+        for i in range(STEP // SUB):
+            n = t * pairs + i // 2
+            if i == 0:
+                for m in range(pairs if moves else 1):
+                    for copy in fetch(n + m):
+                        copy.wait()
+            elif i % 2 == 0 and not moves:
+                for copy in fetch(n):
+                    copy.wait()
+            u = t * (STEP // SUB) + i
+            accs, others = ((a0, a1), (b0, b1)) if i % 2 == 0 else ((b0, b1), (a0, a1))
+            table[u] = drain(others)
+            refs = [flows.at[n], classes.at[n], basins.at[n], depths.at[n]]
+            bin_half(*refs, i % 2, accs, (lambda u=u: move(u - 1)) if moves else None)
+
+    per = STEP // SUB
 
     def step(t, carry):
-        bin_unit_pair(t, lambda: move(2 * t - 1))
-        move(2 * t)
-        for stage, late in ((finish, 3), (finish, 2), (forward, 5), (forward, 4)):
-            from_zero(stage, 2 * t - late)
+        bin_step(t, True)
+        for late in range(per, 0, -1):
+            finish(per * t - late)
+        for late in range(2 * per, per, -1):
+            from_zero(forward, per * t - late)
         return carry
 
-    bin_unit_pair(0, lambda: None)
+    bin_step(0, False)
     pl.semaphore_wait(barrier, len(column) + len(lat_peers))
     load.wait()
-    move(0)
-    lax.fori_loop(1, steps, step, 0)
+    for u in range(per - 1):
+        move(u)
+    lax.fori_loop(1, units // per, step, 0)
     table[units] = drain((b0, b1))
     last = units - 1
-    for stage, u in ((move, last), (finish, last - 2), (forward, last - 4), (finish, last - 1), (forward, last - 3),
-                     (finish, last), (forward, last - 2), (forward, last - 1), (forward, last)):
-        if u >= 0:
-            stage(u)
+    move(last)
+    finish(last - 3)
+    finish(last - 2)
+    for u in range(last - 7, last - 3):
+        forward(u)
+    finish(last - 1)
+    forward(last - 3)
+    finish(last)
+    for u in range(last - 2, last + 1):
+        forward(u)
 
     def settle(u, carry):
         for k in range(1, lats):

time: 53.6 us -> 53.5 us (level)
  no operation moved by 1% of the time
where the time goes in v6:
time: 53.5 us; the launch traced here: 53.4 us
  Pallas kernels  53.2 us (99%)
    pallas_call x1, Pallas kernels, fused(): pl.pallas_call(functools.partial(fused_kernel, lats, lons), out_shape=jax...  52.2 us

profile of v6, /device:TPU:0, one launch (start us, length us, event | category | flops | bytes accessed | tf_op | source)
XLA Modules:
  0.0 53.4 jit_solution(2899323580943452302)
XLA Ops:
  0.0 52.2 %fused_rows.1.in_ref = bf16[64,8,1024]{2,1,0:T(8,128)(2,1)S(1)} custom-call(bf16[48,128,384]{2,1,0:T(8,128)(2,1)} %refs_0_.1, s32[48,128,384]{2,1,0:T(8,128)} %refs_1_.1, s32[128,384]{1,0:T(8,128)} %refs_2_.1, s32[128,384]{1,0:T(8,128)} %refs_3_.1, f8e4m3fn[512,512]{1,0:T(32,128)(4,1)} %constant.2.clone.refs_4_), custom_call_target="tpu_custom_call" | custom-call | tf_op jit(solution)/shard_map/fused_rows/pallas_call | solution.py:292
  52.2 1.0 %turn_rows.1 = bf16[4,200,512]{2,1,0:T(8,128)(2,1)} custom-call(bf16[64,8,1024]{2,1,0:T(8,128)(2,1)S(1)} %fused_rows.1.in_ref), custom_call_target="tpu_custom_call" | custom-call | tf_op jit(solution)/shard_map/turn_rows/pallas_call | solution.py:332
